TPU v7x, 32 devices: a whole 2x2x4 slice. The times are simulated.
32 devices in a mesh: node: 4 (over y, core), local: 8 (over z, x).
Axes of the slice: x: 2, y: 2, z: 4, core: 2. Of those that a mesh axis runs over, the one named last changes fastest.
Arguments:
- tokens: bfloat16 [2048, 7168], P(('node', 'local')), may hold values from -6 to 6
- routes: int32 [2048, 8], P(('node', 'local')), may hold values from 0 to 15, as said below
- gates: bfloat16 [2048, 8], P(('node', 'local')), may hold values from 0.049804688 to 0.5
- w_in: bfloat16 [32, 3584, 2048], P(('node', 'local')), may hold values from -0.0625 to 0.0625
- w_out: bfloat16 [32, 1024, 3584], P(('node', 'local')), may hold values from -0.1875 to 0.1875
Outputs:
- combined: bfloat16 [2048, 7168], P(('node', 'local'))
Inputs may be any that keep to these rules, and one draw needn't show every extreme that they name: `routes`: expert e belongs to node group e // 4. Each row names 8 different experts, 4 in each of exactly 2 node groups. Among the 64 rows of one device no expert is named more than 40 times, and some expert is named exactly 40 times by the rows of every device.
All inputs are finite; a program needn't handle non-finite values.
Results may differ from a plain program's by a relative error of at most 0.011.
Values may be sent and summed in bfloat16 or wider, within the bound.
A program may use at most 128 MiB of HBM per device.

v0:
```python
import jax
import jax.numpy as jnp
from jax import lax
from jax.sharding import PartitionSpec as P


def from_partner(block, axis, stride):
    count = lax.axis_size(axis)
    route = []
    for low in range(count):
        high = low | 1 << stride
        if high != low and high < count:
            route += [(low, high), (high, low)]
    return lax.ppermute(block, axis, route)


def shards(tokens, routes, gates, w_in, w_out):
    tok_count = tokens.shape[0]
    width = tokens.shape[1]
    top_count = routes.shape[1]
    half = width // 2
    device_count = lax.axis_size(("node", "local"))
    expert_count = device_count // 2
    capacity = 5 * tok_count * top_count // (4 * expert_count)
    w_first = w_in[0]
    w_second = w_out[0]
    hidden = w_second.shape[0]
    gate_values = gates.astype(jnp.float32)
    picks = tok_count * top_count
    flat_e = routes.reshape(picks)
    specialist_numbers = jnp.arange(expert_count, dtype=jnp.int32)
    onehot = (flat_e[:, None] == specialist_numbers[None, :]).astype(jnp.int32)
    before = jnp.cumsum(onehot, axis=0) - onehot
    position = jnp.sum(before * onehot, axis=1)
    dest = (flat_e * capacity + position).reshape(tok_count, top_count)
    slot_ids = jnp.arange(expert_count * capacity, dtype=jnp.int32)
    send_match = slot_ids[:, None, None] == dest[None, :, :]
    placing = (
        jnp.any(send_match, axis=2).astype(jnp.bfloat16).reshape(expert_count, capacity, tok_count)
    )
    back_match = dest[:, :, None] == slot_ids[None, None, :]
    weighting = jnp.sum(jnp.where(back_match, gate_values[:, :, None], 0.0), axis=1).astype(
        jnp.bfloat16
    )
    weighting = weighting.reshape(tok_count, expert_count, capacity)
    outgoing = jnp.einsum(
        "ect,thd->ehcd",
        placing,
        tokens.reshape(tok_count, 2, half),
        preferred_element_type=jnp.float32,
    ).astype(jnp.bfloat16)
    outgoing = outgoing.reshape(device_count, capacity, half)
    received = lax.all_to_all(outgoing, ("node", "local"), split_axis=0, concat_axis=0, tiled=True)
    sources = received.shape[0]
    count = received.shape[1]
    partial_value = jnp.dot(
        received.reshape(sources * count, half), w_first, preferred_element_type=jnp.float32
    )
    proj = partial_value + from_partner(partial_value, "local", 0)
    act = (jax.nn.silu(proj[:, :hidden]) * proj[:, hidden:]).astype(jnp.bfloat16)
    returned = lax.all_to_all(
        jnp.dot(act, w_second, preferred_element_type=jnp.float32)
        .astype(jnp.bfloat16)
        .reshape(sources, count, half),
        ("node", "local"),
        split_axis=0,
        concat_axis=0,
        tiled=True,
    )
    returned = returned.reshape(expert_count, 2, capacity, half)
    combined = jnp.einsum("tec,ehcd->thd", weighting, returned, preferred_element_type=jnp.float32)
    return combined.reshape(tok_count, width).astype(jnp.bfloat16)


def solution(mesh):
    return jax.shard_map(
        shards,
        mesh=mesh,
        in_specs=(
            P(("node", "local"), None),
            P(("node", "local"), None),
            P(("node", "local"), None),
            P(("node", "local"), None, None),
            P(("node", "local"), None, None),
        ),
        out_specs=P(("node", "local"), None),
        check_vma=False,
    )
```

profile of v0, /device:TPU:2, one launch (start us, length us, event | category | flops | bytes accessed | tf_op | source)
XLA Modules:
  0.0 742.9 jit_solution(3194727489858603386)
XLA Ops:
  0.0 0.8 copy.39
  1.0 1.2 reduce-window.6
  2.1 0.2 slice_reduce_fusion
  2.4 0.1 fusion.11
  2.5 0.1 reduce_sum.21
  2.6 0.7 multiply_add_fusion
  3.4 0.5 fusion.7
  3.9 0.2 copy.47
  4.1 3.7 convolution_convert_fusion.1
  7.8 206.6 %all_to_all.10 = bf16[32,40,3584]{2,1,0:T(8,128)(2,1)S(1)} all-to-all(bf16[32,40,3584]{2,1,0:T(8,128)(2,1)S(1)} %bitcast.57), channel_id=1, replica_groups=mesh['node'=4,'local'=8] {'node','local'}, dimensions={0} | all-to-all | bytes 18350080 | tf_op jit(solution)/shard_map/all_to_all | solution.py:53
  214.5 22.5 %fusion = f32[1280,2048]{1,0:T(8,128)S(1)} fusion(bf16[1280,3584]{1,0:T(8,128)(2,1)S(1)} %bitcast.60, bf16[1,3584,2048]{2,1,0:T(8,128)(2,1)} %param.8), kind=kOutput, calls=%fused_computation.1 | convolution fusion | flops 18790481920 | bytes 34340864 | tf_op jit(solution)/shard_map/dot_general | solution.py:56
  237.0 3.8 copy-done
  240.8 1.2 collective-permute-start
  242.0 226.4 %collective-permute-done = f32[1280,2048]{1,0:T(8,128)} collective-permute-done((f32[1280,2048]{1,0:T(8,128)S(1)}, f32[1280,2048]{1,0:T(8,128)}, u32[]{:S(2)}, u32[]{:S(2)}) %collective-permute-start) | collective-permute-done | bytes 10485792 | tf_op jit(solution)/shard_map/ppermute | solution.py:14
  468.4 14.5 %add.15 = f32[1280,2048]{1,0:T(8,128)} add(f32[1280,2048]{1,0:T(8,128)} %copy-done, f32[1280,2048]{1,0:T(8,128)} %collective-permute-done) | non-fusion elementwise | flops 2621440 | bytes 31457280 | tf_op jit(solution)/shard_map/add | solution.py:59
  482.8 16.7 %convolution_convert_fusion = bf16[1280,3584]{1,0:T(8,128)(2,1)} fusion(bf16[1,1024,3584]{2,1,0:T(8,128)(2,1)} %param.9, f32[1280,2048]{1,0:T(8,128)} %add.15), kind=kOutput, calls=%fused_computation | convolution fusion | flops 9407692800 | bytes 27000832 | tf_op jit(solution)/shard_map/dot_general | solution.py:62
  499.5 4.2 all-to-all-start.1
  503.7 0.1 copy.44
  503.8 0.5 select_reduce_fusion
  504.2 0.2 copy.45
  504.4 203.1 %all-to-all-done.1 = bf16[32,40,3584]{2,1,0:T(8,128)(2,1)} async-done(((bf16[32,40,3584]{2,1,0:T(8,128)(2,1)}), bf16[32,40,3584]{2,1,0:T(8,128)(2,1)}, u32[]{:S(2)}, u32[]{:S(2)}) %all-to-all-start.1) | async-done | bytes 9175072 | tf_op jit(solution)/shard_map/all_to_all | solution.py:61
  707.5 14.1 %copy.59 = bf16[16,2,40,3584]{3,1,2,0:T(2,128)(2,1)} copy(bf16[16,2,40,3584]{3,2,1,0:T(8,128)(2,1)} %bitcast.12) | data formatting | bytes 18350080 | tf_op jit(solution)/shard_map/reshape | solution.py:70
  721.6 15.1 %dot_general.20 = bf16[7168,40,16]{0,1,2:T(8,128)(2,1)} reshape(bf16[2,3584,40,16]{1,0,2,3:T(2,128)(2,1)} %bitcast.58) | data formatting | bytes 18350080 | tf_op jit(solution)/shard_map/tec,ehcd->thd/dot_general | solution.py:71
  736.7 6.2 fusion.2
  (10 shorter events, 0.4 us)
Async XLA Ops:
  237.0 3.8 copy-start
  240.8 227.5 %collective-permute-start = (f32[1280,2048]{1,0:T(8,128)S(1)}, f32[1280,2048]{1,0:T(8,128)}, u32[]{:S(2)}, u32[]{:S(2)}) collective-permute-start(f32[1280,2048]{1,0:T(8,128)S(1)} %fusion), channel_id=1, source_target_pairs={{0,1},{1,0},{2,3},{3,2},{4,5},{5,4},{6,7},{7,6},{8,9},{9,8},{10,11... | collective-permute-start | bytes 31457288 | tf_op jit(solution)/shard_map/ppermute | solution.py:14
  499.5 4.2 copy-start.1
  499.5 208.0 %all-to-all-start.1 = ((bf16[32,40,3584]{2,1,0:T(8,128)(2,1)}), bf16[32,40,3584]{2,1,0:T(8,128)(2,1)}, u32[]{:S(2)}, u32[]{:S(2)}) async-start(bf16[32,40,3584]{2,1,0:T(8,128)(2,1)} %bitcast.59), calls=%async_computation.1 | async-start | bytes 18350080 | tf_op jit(solution)/shard_map/all_to_all | solution.py:61
where the time goes:
time: 745 us; the launch traced here: 743 us
  waiting for transfers between devices  429 us (58%)
  blocking collectives  207 us (28%)
  matrix products  49.1 us (7%)
  local copies, waits for them, and re-layouts  35 us (5%)
  other arithmetic  17.4 us (2%)
    ppermute x1, waiting for transfers between devices, from_partner(): return lax.ppermute(block, axis, route)  226 us
    all_to_all x1, blocking collectives, shards(): lax.all_to_all(outgoing, ('node', 'local'), split_axis=0, concat_axis=0,...  207 us
    all_to_all x1, waiting for transfers between devices, shards(): lax.all_to_all(jnp.dot(act, w_second, preferred_element_type=jnp.float32)...  203 us
    dot_general x1, matrix products, shards(): jnp.dot(received.reshape(sources * count, half), w_first, preferred_eleme...  22.5 us
    dot_general x1, matrix products, shards(): jnp.dot(act, w_second, preferred_element_type=jnp.float32)  16.7 us
    dot_general x1, local copies, waits for them, and re-layouts, shards(): jnp.einsum('tec,ehcd->thd', weighting, returned, preferred_element_type=j...  15.1 us
  transfers between devices with their start and end apart: 2, of which 2 were waited for; matrix products, arithmetic and copies ran while one was open for 0% of the time, Pallas kernels for 0%

commit v1 on v0

v1 whole, which is shorter than its diff:
```python
import functools

import jax
import jax.numpy as jnp
from jax import lax
from jax.experimental import pallas as pl
from jax.experimental.pallas import tpu as pltpu

MESH = pl.DeviceIdType.MESH


def copy_to(src, dst, send_sem, recv_sem, device):
    return pltpu.make_async_remote_copy(
        src_ref=src,
        dst_ref=dst,
        send_sem=send_sem,
        recv_sem=recv_sem,
        device_id=device,
        device_id_type=MESH,
    )


def place():
    node = lax.axis_index("node")
    local = lax.axis_index("local")
    return node // 2, lax.rem(node, 2), local // 2, lax.rem(local, 2)


def device(y, c, z, x):
    return (y * 2 + c, z * 2 + x)


def greet(ny, m):
    y, c, z, x = place()
    barrier = pltpu.get_barrier_semaphore()

    def hello(dev):
        pl.semaphore_signal(barrier, inc=1, device_id=dev, device_id_type=MESH)

    hello(device(y, c, z, 1 - x))
    hello(device(y, 1 - c, z, x))
    for dy in range(1, ny):
        hello(device(lax.rem(y + dy, ny), c, z, x))

    @pl.when(z > 0)
    def _():
        hello(device(y, c, z - 1, x))

    @pl.when(z < m - 1)
    def _():
        hello(device(y, c, z + 1, x))

    ends = (z > 0).astype(jnp.int32) + (z < m - 1).astype(jnp.int32)
    pl.semaphore_wait(barrier, ny + 1 + ends)


def gather_kernel(q, ny, m, tok_ref, buf_ref, loc_sem, pair_sem, recv, zsend, ysend, csend):
    y, c, z, x = place()
    greet(ny, m)
    partner = device(y, c, z, 1 - x)

    def slab(yy, cc, zz):
        return buf_ref.at[yy, cc, zz]

    def arrived(yy, cc, zz):
        s = slab(yy, cc, zz)
        copy_to(s, s, pair_sem, recv.at[yy, cc, zz], partner).wait_recv()

    def up(zz):
        return copy_to(slab(y, c, zz), slab(y, c, zz), zsend.at[0, zz], recv.at[y, c, zz],
                       device(y, c, z + 1, x))

    def down(zz):
        return copy_to(slab(y, c, zz), slab(y, c, zz), zsend.at[1, zz], recv.at[y, c, zz],
                       device(y, c, z - 1, x))

    def across(dy, zz):
        return copy_to(slab(y, c, zz), slab(y, c, zz), ysend.at[dy, zz], recv.at[y, c, zz],
                       device(lax.rem(y + dy, ny), c, z, x))

    def core(yy, zz):
        return copy_to(slab(yy, c, zz), slab(yy, c, zz), csend.at[yy, zz], recv.at[yy, c, zz],
                       device(y, 1 - c, z, x))

    mine = pltpu.make_async_copy(tok_ref.at[q], slab(y, c, z), loc_sem)
    give = copy_to(tok_ref.at[1 - q], slab(y, c, z), pair_sem, recv.at[y, c, z], partner)

    @pl.when(x == q)
    def _():
        give.start()
        mine.start()
        mine.wait()

    @pl.when(x != q)
    def _():
        arrived(y, c, z)

    def have(zz, is_up, is_down):
        if is_up:
            @pl.when(z + 1 < m)
            def _():
                up(zz).start()
        if is_down:
            @pl.when(z > 0)
            def _():
                down(zz).start()
        for dy in range(1, ny):
            across(dy, zz).start()
        core(y, zz).start()

    def relay(zz):
        for dy in range(1, ny):
            yy = lax.rem(y + dy, ny)
            arrived(yy, c, zz)
            core(yy, zz).start()

    def both(s, act):
        if s == 0:
            act(z, True, True)
            return

        @pl.when(z - s >= 0)
        def _():
            act(z - s, True, False)

        @pl.when(z + s < m)
        def _():
            act(z + s, False, True)

    have(z, True, True)
    for s in range(1, m):
        def first(zz, is_up, is_down):
            arrived(y, c, zz)
            have(zz, is_up, is_down)

        both(s, first)
        both(s - 1, lambda zz, u, d: relay(zz))
    both(m - 1, lambda zz, u, d: relay(zz))

    @pl.when(x == q)
    def _():
        give.wait_send()

    for yy in range(ny):
        for zz in range(m):
            arrived(yy, 1 - c, zz)
            core(yy, zz).wait_send()
    for zz in range(m):
        for dy in range(1, ny):
            across(dy, zz).wait_send()

        @pl.when((z + 1 < m) & (z >= zz))
        def _():
            up(zz).wait_send()

        @pl.when((z > 0) & (z <= zz))
        def _():
            down(zz).wait_send()


def add_into(acc, other):
    rows = acc.shape[0]

    @pl.loop(0, rows // 16)
    def _(i):
        r = pl.ds(pl.multiple_of(i * 16, 16), 16)
        acc[r, :] = (acc[r, :].astype(jnp.float32) + other[r, :].astype(jnp.float32)).astype(
            acc.dtype
        )


def scatter_kernel(q, ny, m, in_ref, out_ref, own, got_c, got_y, got_z, load, csend, crecv,
                   ysend, yrecv, zsend, zrecv, psend, precv, osem):
    y, c, z, x = place()
    greet(ny, m)
    partner = device(y, c, z, 1 - x)

    def core(yy, zz):
        return copy_to(in_ref.at[yy, 1 - c, zz], got_c.at[yy, zz], csend.at[yy, zz],
                       crecv.at[yy, zz], device(y, 1 - c, z, x))

    def fetch(yy, zz):
        return pltpu.make_async_copy(in_ref.at[yy, c, zz], own.at[yy, zz], load.at[yy, zz])

    def across(dy, zz):
        return copy_to(own.at[lax.rem(y + dy, ny), zz], got_y.at[y, zz], ysend.at[dy, zz],
                       yrecv.at[y, zz], device(lax.rem(y + dy, ny), c, z, x))

    def up(zz):
        return copy_to(own.at[y, zz], got_z.at[0, zz], zsend.at[0, zz], zrecv.at[0, zz],
                       device(y, c, z + 1, x))

    def down(zz):
        return copy_to(own.at[y, zz], got_z.at[1, zz], zsend.at[1, zz], zrecv.at[1, zz],
                       device(y, c, z - 1, x))

    def far_first(act):
        for s in range(m - 1, 0, -1):
            @pl.when(z + s < m)
            def _():
                act(z + s, 1)

            @pl.when(z - s >= 0)
            def _():
                act(z - s, -1)
        act(z, 0)

    def start_cross(zz, way):
        for dy in range(1, ny):
            yy = lax.rem(y + dy, ny)
            core(yy, zz).start()
            fetch(yy, zz).start()

    def start_own(zz, way):
        core(y, zz).start()
        fetch(y, zz).start()

    far_first(start_cross)
    far_first(start_own)

    def chip_sum(yy, zz):
        fetch(yy, zz).wait()
        core(yy, zz).wait_recv()
        add_into(own.at[yy, zz], got_c.at[yy, zz])

    def send_cross(zz, way):
        for dy in range(1, ny):
            chip_sum(lax.rem(y + dy, ny), zz)
            across(dy, zz).start()

    far_first(send_cross)
    far_first(lambda zz, way: chip_sum(y, zz))

    def from_z(k, zz):
        copy_to(own.at[y, zz], got_z.at[k, zz], zsend.at[k, zz], zrecv.at[k, zz],
                partner).wait_recv()
        add_into(own.at[y, zz], got_z.at[k, zz])

    def line(zz, way):
        for dy in range(1, ny):
            yy = lax.rem(y + dy, ny)
            copy_to(own.at[y, zz], got_y.at[yy, zz], psend, yrecv.at[yy, zz], partner).wait_recv()
            add_into(own.at[y, zz], got_y.at[yy, zz])
        if way >= 0:
            @pl.when(z > 0)
            def _():
                from_z(0, zz)
        if way <= 0:
            @pl.when(z < m - 1)
            def _():
                from_z(1, zz)
        if way > 0:
            up(zz).start()
        if way < 0:
            down(zz).start()

    far_first(line)

    final = own.at[y, z]
    mine = pltpu.make_async_copy(final, out_ref.at[q], osem)
    give = copy_to(final, out_ref.at[1 - q], psend, precv, partner)

    @pl.when(x == q)
    def _():
        mine.start()
        mine.wait()
        give.wait_recv()

    @pl.when(x != q)
    def _():
        give.start()
        give.wait_send()

    for yy in range(ny):
        for zz in range(m):
            core(yy, zz).wait_send()
    for zz in range(m):
        for dy in range(1, ny):
            across(dy, zz).wait_send()

        @pl.when(z < zz)
        def _():
            up(zz).wait_send()

        @pl.when(z > zz)
        def _():
            down(zz).wait_send()


def gather_rows(q, ny, m, tok):
    _, rows, half = tok.shape
    sem = pltpu.SemaphoreType.DMA
    total = ny * 2 * m * rows * half * 2
    return pl.pallas_call(
        functools.partial(gather_kernel, q, ny, m),
        out_shape=jax.ShapeDtypeStruct((ny, 2, m, rows, half), tok.dtype),
        in_specs=[pl.BlockSpec(memory_space=pltpu.VMEM)],
        out_specs=pl.BlockSpec(memory_space=pl.ANY),
        scratch_shapes=[sem, sem, sem((ny, 2, m)), sem((2, m)), sem((ny, m)), sem((ny, m))],
        compiler_params=pltpu.CompilerParams(collective_id=q, has_side_effects=True),
        cost_estimate=pl.CostEstimate(flops=0, bytes_accessed=20 * total, transcendentals=0),
    )(tok)


def scatter_rows(q, ny, m, dense):
    rows, half = dense.shape[-2:]
    sem = pltpu.SemaphoreType.DMA
    vmem = pltpu.VMEM
    total = ny * 2 * m * rows * half * 2
    slab = (rows, half)
    return pl.pallas_call(
        functools.partial(scatter_kernel, q, ny, m),
        out_shape=jax.ShapeDtypeStruct((2, rows, half), dense.dtype),
        in_specs=[pl.BlockSpec(memory_space=pl.ANY)],
        out_specs=pl.BlockSpec(memory_space=pltpu.VMEM),
        scratch_shapes=[
            vmem((ny, m) + slab, dense.dtype),
            vmem((ny, m) + slab, dense.dtype),
            vmem((ny, m) + slab, dense.dtype),
            vmem((2, m) + slab, dense.dtype),
            sem((ny, m)),
            sem((ny, m)),
            sem((ny, m)),
            sem((ny, m)),
            sem((ny, m)),
            sem((2, m)),
            sem((2, m)),
            sem,
            sem,
            sem,
        ],
        compiler_params=pltpu.CompilerParams(
            collective_id=2 + q, has_side_effects=True, vmem_limit_bytes=62 * 1024 * 1024
        ),
        cost_estimate=pl.CostEstimate(flops=0, bytes_accessed=20 * total, transcendentals=0),
    )(dense)


def from_partner(block, axis):
    count = lax.axis_size(axis)
    return lax.ppermute(block, axis, [(i, i ^ 1) for i in range(count)])


def shards(tokens, routes, gates, w_in, w_out):
    rows, width = tokens.shape
    top = routes.shape[1]
    half = width // 2
    nodes = lax.axis_size("node")
    locals_ = lax.axis_size("local")
    ny, m = nodes // 2, locals_ // 2
    experts = nodes * m
    cap = 5 * rows * top // (4 * experts)
    w_first, w_second = w_in[0], w_out[0]
    hidden = w_second.shape[0]
    x = lax.rem(lax.axis_index("local"), 2)
    expert = (lax.axis_index("node") * locals_ + lax.axis_index("local")) // 2

    info = jnp.concatenate([routes.astype(jnp.bfloat16), gates], axis=1)
    info = lax.all_gather(info, ("node", "local"), axis=0, tiled=True)
    info = info.reshape(experts, 2, rows, 2 * top).astype(jnp.float32)
    named = info[..., :top] == expert.astype(jnp.float32)
    gate = jnp.sum(jnp.where(named, info[..., top:], 0.0), axis=3)
    chosen = jnp.any(named, axis=3)
    count = jnp.cumsum(chosen.astype(jnp.int32), axis=2) - 1
    slots = jnp.arange(cap, dtype=jnp.int32)
    match = chosen[:, :, None, :] & (count[:, :, None, :] == slots[None, None, :, None])
    placing = match.astype(jnp.bfloat16)
    weighting = jnp.where(match, gate[:, :, None, :], 0.0).astype(jnp.bfloat16)

    tok = tokens.reshape(rows, 2, half).transpose(1, 0, 2)
    parts = []
    for q in range(2):
        buf = gather_rows(q, ny, m, tok).reshape(experts, rows, half)
        picked = jnp.einsum(
            "bct,bth->bch", placing[:, q], buf, preferred_element_type=jnp.float32
        ).astype(jnp.bfloat16)
        part = jnp.dot(
            picked.reshape(experts * cap, half), w_first, preferred_element_type=jnp.float32
        ).astype(jnp.bfloat16)
        if q == 0:
            tok, part = lax.optimization_barrier((tok, part))
        parts.append((part, from_partner(part, "local")))
    outs = []
    for q in range(2):
        part, other = parts[q]
        proj = part.astype(jnp.float32) + other.astype(jnp.float32)
        act = (jax.nn.silu(proj[:, :hidden]) * proj[:, hidden:]).astype(jnp.bfloat16)
        result = jnp.dot(act, w_second, preferred_element_type=jnp.float32).astype(jnp.bfloat16)
        dense = jnp.einsum(
            "bct,bch->bth",
            weighting[:, q],
            result.reshape(experts, cap, half),
            preferred_element_type=jnp.float32,
        ).astype(jnp.bfloat16)
        outs.append(scatter_rows(q, ny, m, dense.reshape(ny, 2, m, rows, half)))
    final = jnp.where(x == 0, outs[0], outs[1])
    return final.transpose(1, 0, 2).reshape(rows, width)


def solution(mesh):
    spec = ("node", "local")
    return jax.shard_map(
        shards,
        mesh=mesh,
        in_specs=(
            P2(spec),
            P2(spec),
            P2(spec),
            P3(spec),
            P3(spec),
        ),
        out_specs=P2(spec),
        check_vma=False,
    )


def P2(spec):
    return jax.sharding.PartitionSpec(spec, None)


def P3(spec):
    return jax.sharding.PartitionSpec(spec, None, None)
```

time: 745 us -> 443 us (0.59)
  waiting for transfers between devices: 429 us -> 0.01 us
  Pallas kernels: 0 us -> 253 us
  blocking collectives: 207 us -> 64.7 us
  starting transfers between devices: 5.33 us -> 49.2 us
  local copies, waits for them, and re-layouts: 35 us -> 3.16 us
  matrix products: 49.1 us -> 63.1 us
  other arithmetic: 17.4 us -> 9.92 us
    pallas_call x0 -> x4, Pallas kernels: none -> 253 us  [the longest x2 129 us: gather_rows(): pl.pallas_call(functools.partial(gather_kernel, q, ny, m), out_shape=jax....]
    ppermute x1 -> x2, waiting for transfers between devices: 226 us -> 0.01 us  [from_partner(): return lax.ppermute(block, axis, [(i, i ^ 1) for i in range(count)])]
    all_to_all x1 -> x0, blocking collectives: 207 us -> none  [shards(): lax.all_to_all(outgoing, ('node', 'local'), split_axis=0, concat_axis=0,...]
    all_to_all x1 -> x0, waiting for transfers between devices: 203 us -> none  [shards(): lax.all_to_all(jnp.dot(act, w_second, preferred_element_type=jnp.float32)...]
    all_gather x0 -> x1, blocking collectives: none -> 64.7 us  [shards(): info = lax.all_gather(info, ('node', 'local'), axis=0, tiled=True)]
    ppermute x1 -> x2, starting transfers between devices: 1.17 us -> 49.2 us  [from_partner(): return lax.ppermute(block, axis, [(i, i ^ 1) for i in range(count)])]
    dot_general x1 -> x0, local copies, waits for them, and re-layouts: 15.1 us -> none  [shards(): jnp.einsum('tec,ehcd->thd', weighting, returned, preferred_element_type=j...]
    dot_general x3 -> x6, matrix products: 32.5 us -> 46.6 us  [the longest x2 27.6 us: shards(): jnp.dot(picked.reshape(experts * cap, half), w_first, preferred_element_t...]
  transfers between devices with their start and end apart: 2 -> 2, of which waited for: 2 -> 0; matrix products, arithmetic and copies ran while one was open for 0% -> 8% of each run, Pallas kernels for 0% -> 29%
where the time goes in v1:
time: 443 us
  Pallas kernels  253 us (57%)
  blocking collectives  64.7 us (15%)
  matrix products  63.1 us (14%)
  starting transfers between devices  49.2 us (11%)
  other arithmetic  9.92 us (2%)
    pallas_call x2, Pallas kernels, gather_rows(): pl.pallas_call(functools.partial(gather_kernel, q, ny, m), out_shape=jax....  129 us
    pallas_call x2, Pallas kernels, scatter_rows(): pl.pallas_call(functools.partial(scatter_kernel, q, ny, m), out_shape=jax...  124 us
    all_gather x1, blocking collectives, shards(): info = lax.all_gather(info, ('node', 'local'), axis=0, tiled=True)  64.7 us
    ppermute x2, starting transfers between devices, from_partner(): return lax.ppermute(block, axis, [(i, i ^ 1) for i in range(count)])  49.2 us
    dot_general x2, matrix products, shards(): jnp.dot(picked.reshape(experts * cap, half), w_first, preferred_element_t...  27.6 us
    dot_general x2, matrix products, shards(): jnp.dot(act, w_second, preferred_element_type=jnp.float32)  16.4 us
    dot_general x2, matrix products, shards(): jnp.einsum('bct,bch->bth', weighting[:, q], result.reshape(experts, cap,...  10.2 us
  transfers between devices with their start and end apart: 2, of which 0 were waited for; matrix products, arithmetic and copies ran while one was open for 8% of the time, Pallas kernels for 29%

profile of v1, /device:TPU:2, one launch (start us, length us, event | category | flops | bytes accessed | tf_op | source)
XLA Modules:
  0.0 443.0 jit_solution(15433282861455978710)
XLA Ops:
  0.0 0.7 convert_element_type.65
  0.7 0.7 maximum_bitcast_fusion
  1.4 64.7 %all-gather = bf16[32,64,16]{1,2,0:T(8,128)(2,1)S(1)} all-gather(bf16[1,64,16]{1,2,0:T(8,128)(2,1)S(1)} %maximum_bitcast_fusion), channel_id=1, replica_groups=mesh['node'=4,'local'=8] {'node','local'}, dimensions={0}, use_global_device_ids=true | all-gather | bytes 67584 | tf_op jit(solution)/shard_map/all_gather | solution.py:359
  66.2 0.5 reduce_window_sum.11
  66.7 2.2 copy.22
  68.9 61.5 %shard_map.55 = bf16[2,2,4,64,3584]{4,3,2,1,0:T(8,128)(2,1)} custom-call(bf16[2,64,3584]{2,1,0:T(8,128)(2,1)} %bitcast.66), custom_call_target="tpu_custom_call" | custom-call | bytes 146800640 | tf_op jit(solution)/shard_map/pallas_call | solution.py:294
  130.4 0.1 fusion.26
  130.5 4.4 convolution_convert_fusion.3
  134.9 13.2 %fusion.14 = bf16[640,2048]{1,0:T(8,128)(2,1)S(1)} fusion(bf16[640,3584]{1,0:T(8,128)(2,1)S(1)} %bitcast.65, bf16[1,3584,2048]{2,1,0:T(8,128)(2,1)} %param.8), kind=kOutput, calls=%fused_computation.16 | convolution fusion | flops 9396551680 | bytes 21889024 | tf_op jit(solution)/shard_map/dot_general | solution.py:377
  148.3 67.2 %shard_map.57 = bf16[2,2,4,64,3584]{4,3,2,1,0:T(8,128)(2,1)} custom-call(bf16[2,64,3584]{2,1,0:T(8,128)(2,1)} %bitcast.67), custom_call_target="tpu_custom_call" | custom-call | bytes 146800640 | tf_op jit(solution)/shard_map/pallas_call | solution.py:294
  215.5 4.4 convolution_convert_fusion.2
  219.9 14.4 %fusion.17 = bf16[640,2048]{1,0:T(8,128)(2,1)} fusion(bf16[640,3584]{1,0:T(8,128)(2,1)S(1)} %bitcast.64, bf16[1,3584,2048]{2,1,0:T(8,128)(2,1)} %param.8), kind=kOutput, calls=%fused_computation.17 | convolution fusion | flops 9396551680 | bytes 21889024 | tf_op jit(solution)/shard_map/dot_general | solution.py:377
  234.2 49.1 %collective-permute-start.1 = (bf16[640,2048]{1,0:T(8,128)(2,1)}, bf16[640,2048]{1,0:T(8,128)(2,1)}, u32[]{:S(2)}, u32[]{:S(2)}) collective-permute-start(bf16[640,2048]{1,0:T(8,128)(2,1)} %fusion.17), channel_id=1, source_target_pairs={{0,1},{1,0},{2,3},{3,2},{4,5},{5,4},{6,7},{7,6},{8,9},{9,8},{10,11... | collective-permute-start | bytes 7864328 | tf_op jit(solution)/shard_map/ppermute | solution.py:341
  283.3 0.2 select_convert_fusion
  283.5 2.7 convert_add_fusion.1
  286.3 8.2 %fusion.8 = bf16[640,3584]{1,0:T(8,128)(2,1)S(1)} fusion(bf16[1,1024,3584]{2,1,0:T(8,128)(2,1)} %param.9, f32[640,2048]{1,0:T(8,128)S(1)} %convert_add_fusion.1), kind=kOutput, calls=%fused_computation.10 | convolution fusion | flops 4703846400 | bytes 17170432 | tf_op jit(solution)/shard_map/dot_general | solution.py:388
  294.5 5.1 %convolution_convert_fusion.1 = bf16[16,64,3584]{2,1,0:T(8,128)(2,1)} fusion(bf16[16,40,3584]{2,1,0:T(8,128)(2,1)S(1)} %bitcast.69, bf16[16,2,40,64]{3,2,0,1:T(8,128)(2,1)S(1)} %select_convert_fusion), kind=kOutput, calls=%fused_computation.5 | convolution fusion | flops 297271296 | bytes 12091392 | tf_op jit(solution)/shard_map/bct,bch->bth/dot_general | solution.py:389
  299.6 60.6 %shard_map.56 = bf16[2,64,3584]{2,1,0:T(8,128)(2,1)} custom-call(bf16[2,2,4,64,3584]{4,3,2,1,0:T(8,128)(2,1)} %bitcast.63), custom_call_target="tpu_custom_call" | custom-call | bytes 146800640 | tf_op jit(solution)/shard_map/pallas_call | solution.py:311
  360.2 3.6 convert_add_fusion
  363.8 8.2 %fusion.11 = bf16[640,3584]{1,0:T(8,128)(2,1)S(1)} fusion(bf16[1,1024,3584]{2,1,0:T(8,128)(2,1)} %param.9, f32[640,2048]{1,0:T(8,128)S(1)} %convert_add_fusion), kind=kOutput, calls=%fused_computation.11 | convolution fusion | flops 4703846400 | bytes 17170432 | tf_op jit(solution)/shard_map/dot_general | solution.py:388
  372.0 5.1 %convolution_convert_fusion = bf16[16,64,3584]{2,1,0:T(8,128)(2,1)} fusion(bf16[16,40,3584]{2,1,0:T(8,128)(2,1)S(1)} %bitcast.68, bf16[16,2,40,64]{3,2,0,1:T(8,128)(2,1)S(1)} %select_convert_fusion), kind=kOutput, calls=%fused_computation.4 | convolution fusion | flops 297271296 | bytes 12091392 | tf_op jit(solution)/shard_map/bct,bch->bth/dot_general | solution.py:389
  377.1 63.6 %shard_map.58 = bf16[2,64,3584]{2,1,0:T(8,128)(2,1)} custom-call(bf16[2,2,4,64,3584]{4,3,2,1,0:T(8,128)(2,1)} %bitcast.62), custom_call_target="tpu_custom_call" | custom-call | bytes 146800640 | tf_op jit(solution)/shard_map/pallas_call | solution.py:311
  440.7 1.3 select_bitcast_fusion
  442.0 1.0 copy.19
  (11 shorter events, 0.2 us)
Async XLA Ops:
  148.2 135.3 %collective-permute-start = (bf16[640,2048]{1,0:T(8,128)(2,1)S(1)}, bf16[640,2048]{1,0:T(8,128)(2,1)}, u32[]{:S(2)}, u32[]{:S(2)}) collective-permute-start(bf16[640,2048]{1,0:T(8,128)(2,1)S(1)} %fusion.14), channel_id=1, source_target_pairs={{0,1},{1,0},{2,3},{3,2},{4,5},{5,4},{6,7},{7,6},{8,9},{9,8},{10,11... | collective-permute-start | bytes 7864328 | tf_op jit(solution)/shard_map/ppermute | solution.py:341
  234.2 125.9 %collective-permute-start.1 = (bf16[640,2048]{1,0:T(8,128)(2,1)}, bf16[640,2048]{1,0:T(8,128)(2,1)}, u32[]{:S(2)}, u32[]{:S(2)}) collective-permute-start(bf16[640,2048]{1,0:T(8,128)(2,1)} %fusion.17), channel_id=1, source_target_pairs={{0,1},{1,0},{2,3},{3,2},{4,5},{5,4},{6,7},{7,6},{8,9},{9,8},{10,11... | collective-permute-start | bytes 7864328 | tf_op jit(solution)/shard_map/ppermute | solution.py:341
  377.1 63.6 %copy-start = (bf16[2,64,3584]{2,1,0:T(8,128)(2,1)S(1)}, bf16[2,64,3584]{2,1,0:T(8,128)(2,1)}, u32[]{:S(2)}) copy-start(bf16[2,64,3584]{2,1,0:T(8,128)(2,1)} %shard_map.56) | copy-start | bytes 2752516

commit v2 on v1

--- a/solution.py
+++ b/solution.py
@@ -30,14 +30,15 @@
     return (y * 2 + c, z * 2 + x)
 
 
-def greet(ny, m):
+def greet(ny, m, pair=True):
     y, c, z, x = place()
     barrier = pltpu.get_barrier_semaphore()
 
     def hello(dev):
         pl.semaphore_signal(barrier, inc=1, device_id=dev, device_id_type=MESH)
 
-    hello(device(y, c, z, 1 - x))
+    if pair:
+        hello(device(y, c, z, 1 - x))
     hello(device(y, 1 - c, z, x))
     for dy in range(1, ny):
         hello(device(lax.rem(y + dy, ny), c, z, x))
@@ -51,12 +52,16 @@
         hello(device(y, c, z + 1, x))
 
     ends = (z > 0).astype(jnp.int32) + (z < m - 1).astype(jnp.int32)
-    pl.semaphore_wait(barrier, ny + 1 + ends)
-
-
-def gather_kernel(q, ny, m, tok_ref, buf_ref, loc_sem, pair_sem, recv, zsend, ysend, csend):
+    pl.semaphore_wait(barrier, ny + int(pair) + ends)
+
+
+def gather_kernel(q, ny, m, tok_ref, buf_ref, *rest):
+    if q == 0:
+        seed_ref, loc_sem, pair_sem, seed_sem, recv, zsend, ysend, csend = rest
+    else:
+        loc_sem, pair_sem, recv, zsend, ysend, csend = rest
     y, c, z, x = place()
-    greet(ny, m)
+    greet(ny, m, q == 0)
     partner = device(y, c, z, 1 - x)
 
     def slab(yy, cc, zz):
@@ -82,18 +87,28 @@
         return copy_to(slab(yy, c, zz), slab(yy, c, zz), csend.at[yy, zz], recv.at[yy, c, zz],
                        device(y, 1 - c, z, x))
 
-    mine = pltpu.make_async_copy(tok_ref.at[q], slab(y, c, z), loc_sem)
-    give = copy_to(tok_ref.at[1 - q], slab(y, c, z), pair_sem, recv.at[y, c, z], partner)
-
-    @pl.when(x == q)
-    def _():
-        give.start()
+    if q == 0:
+        mine = pltpu.make_async_copy(tok_ref.at[0], slab(y, c, z), loc_sem)
+        give = copy_to(tok_ref.at[1], slab(y, c, z), pair_sem, recv.at[y, c, z], partner)
+        keep_seed = pltpu.make_async_copy(tok_ref.at[1], seed_ref, loc_sem)
+        give_seed = copy_to(tok_ref.at[0], seed_ref, pair_sem, seed_sem, partner)
+
+        @pl.when(x == 0)
+        def _():
+            give.start()
+            mine.start()
+            mine.wait()
+
+        @pl.when(x != 0)
+        def _():
+            give_seed.start()
+            keep_seed.start()
+            keep_seed.wait()
+            arrived(y, c, z)
+    else:
+        mine = pltpu.make_async_copy(tok_ref, slab(y, c, z), loc_sem)
         mine.start()
         mine.wait()
-
-    @pl.when(x != q)
-    def _():
-        arrived(y, c, z)
 
     def have(zz, is_up, is_down):
         if is_up:
@@ -137,9 +152,15 @@
         both(s - 1, lambda zz, u, d: relay(zz))
     both(m - 1, lambda zz, u, d: relay(zz))
 
-    @pl.when(x == q)
-    def _():
-        give.wait_send()
+    if q == 0:
+        @pl.when(x == 0)
+        def _():
+            give.wait_send()
+            give_seed.wait_recv()
+
+        @pl.when(x != 0)
+        def _():
+            give_seed.wait_send()
 
     for yy in range(ny):
         for zz in range(m):
@@ -288,15 +309,20 @@
 
 
 def gather_rows(q, ny, m, tok):
-    _, rows, half = tok.shape
+    rows, width = tok.shape[-2:]
     sem = pltpu.SemaphoreType.DMA
-    total = ny * 2 * m * rows * half * 2
+    total = ny * 2 * m * rows * width * 2
+    shape = jax.ShapeDtypeStruct((ny, 2, m, rows, width), tok.dtype)
+    anywhere = pl.BlockSpec(memory_space=pl.ANY)
+    vmem = pl.BlockSpec(memory_space=pltpu.VMEM)
+    seed = jax.ShapeDtypeStruct((rows, width), tok.dtype)
+    sems = [sem, sem] + [sem] * (q == 0)
     return pl.pallas_call(
         functools.partial(gather_kernel, q, ny, m),
-        out_shape=jax.ShapeDtypeStruct((ny, 2, m, rows, half), tok.dtype),
-        in_specs=[pl.BlockSpec(memory_space=pltpu.VMEM)],
-        out_specs=pl.BlockSpec(memory_space=pl.ANY),
-        scratch_shapes=[sem, sem, sem((ny, 2, m)), sem((2, m)), sem((ny, m)), sem((ny, m))],
+        out_shape=(shape, seed) if q == 0 else shape,
+        in_specs=[vmem],
+        out_specs=(anywhere, vmem) if q == 0 else anywhere,
+        scratch_shapes=sems + [sem((ny, 2, m)), sem((2, m)), sem((ny, m)), sem((ny, m))],
         compiler_params=pltpu.CompilerParams(collective_id=q, has_side_effects=True),
         cost_estimate=pl.CostEstimate(flops=0, bytes_accessed=20 * total, transcendentals=0),
     )(tok)
@@ -355,30 +381,38 @@
     x = lax.rem(lax.axis_index("local"), 2)
     expert = (lax.axis_index("node") * locals_ + lax.axis_index("local")) // 2
 
+    lanes = 128 * ((2 * top + 127) // 128)
     info = jnp.concatenate([routes.astype(jnp.bfloat16), gates], axis=1)
-    info = lax.all_gather(info, ("node", "local"), axis=0, tiled=True)
-    info = info.reshape(experts, 2, rows, 2 * top).astype(jnp.float32)
-    named = info[..., :top] == expert.astype(jnp.float32)
-    gate = jnp.sum(jnp.where(named, info[..., top:], 0.0), axis=3)
-    chosen = jnp.any(named, axis=3)
-    count = jnp.cumsum(chosen.astype(jnp.int32), axis=2) - 1
+    info = jnp.pad(info, ((0, 0), (0, lanes - 2 * top)))
+    tok = jnp.stack(
+        [jnp.concatenate([tokens[:, h * half : (h + 1) * half], info], axis=1) for h in range(2)]
+    )
     slots = jnp.arange(cap, dtype=jnp.int32)
-    match = chosen[:, :, None, :] & (count[:, :, None, :] == slots[None, None, :, None])
-    placing = match.astype(jnp.bfloat16)
-    weighting = jnp.where(match, gate[:, :, None, :], 0.0).astype(jnp.bfloat16)
-
-    tok = tokens.reshape(rows, 2, half).transpose(1, 0, 2)
-    parts = []
+    parts, weights = [], []
     for q in range(2):
-        buf = gather_rows(q, ny, m, tok).reshape(experts, rows, half)
+        if q == 0:
+            buf, seed = gather_rows(q, ny, m, tok)
+        else:
+            buf = gather_rows(q, ny, m, seed)
+        buf = buf.reshape(experts, rows, half + lanes)
+        info = buf[..., half : half + 2 * top].astype(jnp.float32)
+        named = info[..., :top] == expert.astype(jnp.float32)
+        gate = jnp.sum(jnp.where(named, info[..., top:], 0.0), axis=2)
+        chosen = jnp.any(named, axis=2)
+        count = jnp.cumsum(chosen.astype(jnp.int32), axis=1) - 1
+        match = chosen[:, None, :] & (count[:, None, :] == slots[None, :, None])
+        weights.append(jnp.where(match, gate[:, None, :], 0.0).astype(jnp.bfloat16))
         picked = jnp.einsum(
-            "bct,bth->bch", placing[:, q], buf, preferred_element_type=jnp.float32
+            "bct,bth->bch",
+            match.astype(jnp.bfloat16),
+            buf[..., :half],
+            preferred_element_type=jnp.float32,
         ).astype(jnp.bfloat16)
         part = jnp.dot(
             picked.reshape(experts * cap, half), w_first, preferred_element_type=jnp.float32
         ).astype(jnp.bfloat16)
         if q == 0:
-            tok, part = lax.optimization_barrier((tok, part))
+            seed, part = lax.optimization_barrier((seed, part))
         parts.append((part, from_partner(part, "local")))
     outs = []
     for q in range(2):
@@ -388,7 +422,7 @@
         result = jnp.dot(act, w_second, preferred_element_type=jnp.float32).astype(jnp.bfloat16)
         dense = jnp.einsum(
             "bct,bch->bth",
-            weighting[:, q],
+            weights[q],
             result.reshape(experts, cap, half),
             preferred_element_type=jnp.float32,
         ).astype(jnp.bfloat16)

time: 443 us -> 318 us (0.72)
  blocking collectives: 64.7 us -> 0 us
  starting transfers between devices: 49.2 us -> 0.94 us
  Pallas kernels: 253 us -> 237 us
    all_gather x1 -> x0, blocking collectives: 64.7 us -> none  [shards(): info = lax.all_gather(info, ('node', 'local'), axis=0, tiled=True)]
    ppermute x2, starting transfers between devices: 49.2 us -> 0.94 us  [from_partner(): return lax.ppermute(block, axis, [(i, i ^ 1) for i in range(count)])]
    pallas_call x2, Pallas kernels: 129 us -> 112 us  [gather_rows(): pl.pallas_call(functools.partial(gather_kernel, q, ny, m), out_shape=(sha...]
  transfers between devices with their start and end apart: 2 -> 2, of which waited for: 0 -> 0; matrix products, arithmetic and copies ran while one was open for 8% -> 12% of each run, Pallas kernels for 29% -> 35%
where the time goes in v2:
time: 318 us; the launch traced here: 317 us
  Pallas kernels  237 us (75%)
  matrix products  62.4 us (20%)
  other arithmetic  14 us (4%)
    pallas_call x2, Pallas kernels, scatter_rows(): pl.pallas_call(functools.partial(scatter_kernel, q, ny, m), out_shape=jax...  125 us
    pallas_call x2, Pallas kernels, gather_rows(): pl.pallas_call(functools.partial(gather_kernel, q, ny, m), out_shape=(sha...  112 us
    dot_general x2, matrix products, shards(): jnp.dot(picked.reshape(experts * cap, half), w_first, preferred_element_t...  26.9 us
    dot_general x2, matrix products, shards(): jnp.dot(act, w_second, preferred_element_type=jnp.float32)  16.5 us
    dot_general x2, matrix products, shards(): jnp.einsum('bct,bch->bth', weights[q], result.reshape(experts, cap, half)...  10.2 us
    dot_general x2, matrix products, shards(): jnp.einsum('bct,bth->bch', match.astype(jnp.bfloat16), buf[..., :half], p...  8.87 us
  transfers between devices with their start and end apart: 2, of which 0 were waited for; matrix products, arithmetic and copies ran while one was open for 12% of the time, Pallas kernels for 35%

profile of v2, /device:TPU:2, one launch (start us, length us, event | category | flops | bytes accessed | tf_op | source)
XLA Modules:
  0.0 317.0 jit_solution(3174742307288697235)
XLA Ops:
  0.0 0.7 convert_element_type.79
  0.7 0.7 pad_maximum_fusion.1
  1.5 1.2 fusion.63
  2.8 1.0 pad_maximum_fusion.tok_ref
  3.8 61.1 %shard_map.55 = (bf16[2,2,4,64,3712]{4,3,2,1,0:T(8,128)(2,1)}, bf16[64,3712]{1,0:T(8,128)(2,1)}) custom-call(bf16[2,64,3712]{2,1,0:T(8,128)(2,1)} %pad_maximum_fusion.tok_ref), custom_call_target="tpu_custom_call" | custom-call | bytes 152043520 | tf_op jit(solution)/shard_map/pallas_call | solution.py:320
  64.9 1.0 slice_convert_fusion.1
  65.9 0.4 fusion.38
  66.9 4.4 %fusion.18 = bf16[16,40,3584]{2,1,0:T(8,128)(2,1)S(1)} fusion(bf16[16,64,3712]{2,1,0:T(8,128)(2,1)} %bitcast.43, s32[16,64]{1,0:T(8,128)S(1)} %broadcast_add_fusion.1, pred[16,64]{1,0:T(8,128)(4,1)S(1)} %reduce_or.18), kind=kOutput, calls=%fused_computation.16 | convolution fusion | flops 295976960 | bytes 11932672 | tf_op jit(solution)/shard_map/bct,bth->bch/dot_general | solution.py:405
  71.4 12.9 %fusion.24 = bf16[640,2048]{1,0:T(8,128)(2,1)S(1)} fusion(bf16[640,3584]{1,0:T(8,128)(2,1)S(1)} %bitcast.46, bf16[1,3584,2048]{2,1,0:T(8,128)(2,1)} %param.8), kind=kOutput, calls=%fused_computation.20 | convolution fusion | flops 9396551680 | bytes 21889024 | tf_op jit(solution)/shard_map/dot_general | solution.py:411
  84.4 51.3 %shard_map.57 = bf16[2,2,4,64,3712]{4,3,2,1,0:T(8,128)(2,1)} custom-call(bf16[64,3712]{1,0:T(8,128)(2,1)} %get-tuple-element.12.tok_ref), custom_call_target="tpu_custom_call" | custom-call | bytes 152043520 | tf_op jit(solution)/shard_map/pallas_call | solution.py:320
  135.7 1.0 slice_convert_fusion
  137.7 4.4 %fusion.21 = bf16[16,40,3584]{2,1,0:T(8,128)(2,1)S(1)} fusion(bf16[16,64,3712]{2,1,0:T(8,128)(2,1)} %bitcast.39, s32[16,64]{1,0:T(8,128)S(1)} %broadcast_add_fusion, pred[16,64]{1,0:T(8,128)(4,1)S(1)} %reduce_or.19), kind=kOutput, calls=%fused_computation.17 | convolution fusion | flops 295976960 | bytes 11932672 | tf_op jit(solution)/shard_map/bct,bth->bch/dot_general | solution.py:405
  142.1 14.0 %fusion.27 = bf16[640,2048]{1,0:T(8,128)(2,1)} fusion(bf16[640,3584]{1,0:T(8,128)(2,1)S(1)} %bitcast.47, bf16[1,3584,2048]{2,1,0:T(8,128)(2,1)} %param.8), kind=kOutput, calls=%fused_computation.21 | convolution fusion | flops 9396551680 | bytes 21889024 | tf_op jit(solution)/shard_map/dot_general | solution.py:411
  156.1 0.9 collective-permute-start.1
  157.0 2.7 convert_add_fusion.1
  159.7 8.2 %fusion.12 = bf16[640,3584]{1,0:T(8,128)(2,1)S(1)} fusion(bf16[1,1024,3584]{2,1,0:T(8,128)(2,1)} %param.9, f32[640,2048]{1,0:T(8,128)S(1)} %convert_add_fusion.1), kind=kOutput, calls=%fused_computation.14 | convolution fusion | flops 4703846400 | bytes 17170432 | tf_op jit(solution)/shard_map/dot_general | solution.py:422
  167.9 5.1 %convolution_convert_fusion.1 = bf16[16,64,3584]{2,1,0:T(8,128)(2,1)} fusion(bf16[16,40,3584]{2,1,0:T(8,128)(2,1)S(1)} %bitcast.44, bf16[16,64]{1,0:T(8,128)(2,1)S(1)} %get-tuple-element.15, s32[16,64]{1,0:T(8,128)S(1)} %broadcast_add_fusion.1, pred[16,64]{1,0:T(8,128)(4,1)S(1)} %reduce_or.18), kind=kOutput, calls=%fused_computation.5 | convolution fusion | flops 297394176 | bytes 11934720 | tf_op jit(solution)/shard_map/bct,bch->bth/dot_general | solution.py:423
  173.0 60.7 %shard_map.56 = bf16[2,64,3584]{2,1,0:T(8,128)(2,1)} custom-call(bf16[2,2,4,64,3584]{4,3,2,1,0:T(8,128)(2,1)} %bitcast.40), custom_call_target="tpu_custom_call" | custom-call | bytes 146800640 | tf_op jit(solution)/shard_map/pallas_call | solution.py:337
  233.7 3.6 %convert_add_fusion = f32[640,2048]{1,0:T(8,128)S(1)} fusion(bf16[640,2048]{1,0:T(8,128)(2,1)} %collective-permute-done.1, bf16[640,2048]{1,0:T(8,128)(2,1)} %fusion.27), kind=kLoop, calls=%fused_computation.18 | loop fusion | flops 3932160 | bytes 10485760 | tf_op jit(solution)/shard_map/add | solution.py:420
  237.3 8.2 %fusion.15 = bf16[640,3584]{1,0:T(8,128)(2,1)S(1)} fusion(bf16[1,1024,3584]{2,1,0:T(8,128)(2,1)} %param.9, f32[640,2048]{1,0:T(8,128)S(1)} %convert_add_fusion), kind=kOutput, calls=%fused_computation.15 | convolution fusion | flops 4703846400 | bytes 17170432 | tf_op jit(solution)/shard_map/dot_general | solution.py:422
  245.6 5.1 %convolution_convert_fusion = bf16[16,64,3584]{2,1,0:T(8,128)(2,1)} fusion(bf16[16,40,3584]{2,1,0:T(8,128)(2,1)S(1)} %bitcast.45, bf16[16,64]{1,0:T(8,128)(2,1)S(1)} %get-tuple-element.13, s32[16,64]{1,0:T(8,128)S(1)} %broadcast_add_fusion, pred[16,64]{1,0:T(8,128)(4,1)S(1)} %reduce_or.19), kind=kOutput, calls=%fused_computation.4 | convolution fusion | flops 297394176 | bytes 11934720 | tf_op jit(solution)/shard_map/bct,bch->bth/dot_general | solution.py:423
  250.6 64.1 %shard_map.58 = bf16[2,64,3584]{2,1,0:T(8,128)(2,1)} custom-call(bf16[2,2,4,64,3584]{4,3,2,1,0:T(8,128)(2,1)} %bitcast.41), custom_call_target="tpu_custom_call" | custom-call | bytes 146800640 | tf_op jit(solution)/shard_map/pallas_call | solution.py:337
  314.7 1.3 select_bitcast_fusion
  316.0 1.0 copy.13
  (16 shorter events, 1.8 us)
Async XLA Ops:
  84.3 72.7 %collective-permute-start = (bf16[640,2048]{1,0:T(8,128)(2,1)S(1)}, bf16[640,2048]{1,0:T(8,128)(2,1)}, u32[]{:S(2)}, u32[]{:S(2)}) collective-permute-start(bf16[640,2048]{1,0:T(8,128)(2,1)S(1)} %fusion.24), channel_id=1, source_target_pairs={{0,1},{1,0},{2,3},{3,2},{4,5},{5,4},{6,7},{7,6},{8,9},{9,8},{10,11... | collective-permute-start | bytes 7864328 | tf_op jit(solution)/shard_map/ppermute | solution.py:367
  156.1 77.6 %collective-permute-start.1 = (bf16[640,2048]{1,0:T(8,128)(2,1)}, bf16[640,2048]{1,0:T(8,128)(2,1)}, u32[]{:S(2)}, u32[]{:S(2)}) collective-permute-start(bf16[640,2048]{1,0:T(8,128)(2,1)} %fusion.27), channel_id=1, source_target_pairs={{0,1},{1,0},{2,3},{3,2},{4,5},{5,4},{6,7},{7,6},{8,9},{9,8},{10,11... | collective-permute-start | bytes 7864328 | tf_op jit(solution)/shard_map/ppermute | solution.py:367
  250.6 64.1 %copy-start = (bf16[2,64,3584]{2,1,0:T(8,128)(2,1)S(1)}, bf16[2,64,3584]{2,1,0:T(8,128)(2,1)}, u32[]{:S(2)}) copy-start(bf16[2,64,3584]{2,1,0:T(8,128)(2,1)} %shard_map.56) | copy-start | bytes 2752516
